TPU v7x, 32 devices: a whole 2x2x4 slice. The times are simulated.
32 devices in a mesh: grp: 4 (over x, core), bn: 8 (over z, y).
Axes of the slice: x: 2, y: 2, z: 4, core: 2. Of those that a mesh axis runs over, the one named last changes fastest.
Arguments:
- images: bfloat16 [16, 32, 64, 1024], P('grp', 'bn'), parts along dimension 0, may hold values from -64 to 64
- w_reduce: bfloat16 [1024, 256], replicated, may hold values from -0.1875 to 0.1875
- w_spatial: bfloat16 [3, 3, 256, 256], replicated, may hold values from -0.125 to 0.125
- w_expand: bfloat16 [256, 1024], replicated, may hold values from -0.375 to 0.375
- gain_first: float32 [256], replicated, may hold values from 0.25 to 1.75
- shift_first: float32 [256], replicated, may hold values from -3 to 3
- gain_middle: float32 [256], replicated, may hold values from 0.25 to 1.75
- shift_middle: float32 [256], replicated, may hold values from -3 to 3
- gain_last: float32 [1024], replicated, may hold values from 0.25 to 1.75
- shift_last: float32 [1024], replicated, may hold values from -3 to 3
Outputs:
- block_out: bfloat16 [16, 32, 64, 1024], P('grp', 'bn'), parts along dimension 0
There are 4 independent parts, one for each index of `grp`. A program takes and returns all parts, laid end to end along the dimension named above; an argument that names none is the same for every part. Nothing has to cross between parts.
All inputs are finite; a program needn't handle non-finite values.
Results may differ from a plain program's by a relative error of at most 0.0034.
Values may be sent and summed in bfloat16 or wider, within the bound.
A program may use at most 64 MiB of HBM per device.

v0:
```python
import jax
import jax.numpy as jnp
from jax import lax
from jax.sharding import PartitionSpec as P

epsilon = 1e-05


def padded_2(cells, sides, width):
    for axis, dim in sides:
        count = lax.axis_size(axis)
        ends = count - 1
        head = lax.slice_in_dim(cells, 0, width, axis=dim)
        tail = lax.slice_in_dim(cells, cells.shape[dim] - width, cells.shape[dim], axis=dim)
        cells = jnp.concatenate(
            [
                lax.ppermute(tail, axis, [(i, (i + 1) % count) for i in range(ends)]),
                cells,
                lax.ppermute(head, axis, [((i + 1) % count, i) for i in range(ends)]),
            ],
            axis=dim,
        )
    return cells


def group_sum(partial_value):
    gathered = lax.all_gather(partial_value[None], "bn", axis=0, tiled=True)
    return jnp.sum(gathered, axis=0)


def statistics(values, population):
    pooled_axes = (0, 1, 2)
    moments = group_sum(
        jnp.stack([jnp.sum(values, axis=pooled_axes), jnp.sum(values * values, axis=pooled_axes)])
    )
    average = moments[0] / population
    spread = moments[1] / population - average * average
    return (average, spread)


def apply_norm(values, average, spread, gain, shift):
    return (values - average) * (gain * lax.rsqrt(spread + epsilon)) + shift


def normalize(values, gain, shift, population):
    average, spread = statistics(values, population)
    return apply_norm(values, average, spread, gain, shift)


def body(
    images,
    w_reduce,
    w_spatial,
    w_expand,
    gain_first,
    shift_first,
    gain_middle,
    shift_middle,
    gain_last,
    shift_last,
):
    population = images.shape[0] * images.shape[1] * images.shape[2] * lax.axis_size("bn")
    first = jnp.einsum("nhwc,cd->nhwd", images, w_reduce, preferred_element_type=jnp.float32)
    hidden_first = jax.nn.relu(normalize(first, gain_first, shift_first, population)).astype(
        jnp.bfloat16
    )
    padded = padded_2(hidden_first, (("bn", 1),), 1)
    middle = lax.conv_general_dilated(
        padded,
        w_spatial,
        (1, 1),
        ((0, 0), (1, 1)),
        dimension_numbers=("NHWC", "HWIO", "NHWC"),
        preferred_element_type=jnp.float32,
    )
    hidden_middle = jax.nn.relu(normalize(middle, gain_middle, shift_middle, population)).astype(
        jnp.bfloat16
    )
    last = jnp.einsum("nhwc,cd->nhwd", hidden_middle, w_expand, preferred_element_type=jnp.float32)
    summed = normalize(last, gain_last, shift_last, population) + images.astype(jnp.float32)
    return jax.nn.relu(summed).astype(jnp.bfloat16)


def solution(mesh):
    placed = (P("grp", "bn", None, None), P(), P(), P(), P(), P(), P(), P(), P(), P())
    return jax.shard_map(
        body, mesh=mesh, in_specs=placed, out_specs=P("grp", "bn", None, None), check_vma=False
    )
```

profile of v0, /device:TPU:0, one launch (start us, length us, event | category | flops | bytes accessed | tf_op | source)
XLA Modules:
  0.0 109.6 jit_solution(15792899870236382812)
XLA Ops:
  0.0 0.0 copy-start
  0.0 0.0 copy-start.6
  0.0 0.0 copy-start.8
  0.0 2.5 %fusion.9 = (f32[256]{0:T(256)S(1)}, f32[256]{0:T(256)S(1)}, f32[4,4,64,256]{3,2,1,0:T(8,128)S(1)}) fusion(bf16[4,4,64,1024]{3,2,1,0:T(8,128)(2,1)} %param.10, bf16[1024,256]{1,0:T(8,128)(2,1)} %param.11), kind=kOutput, calls=%fused_computation.32 | convolution fusion | flops 537656832 | bytes 3672064 | tf_op jit(solution)/shard_map/nhwc,cd->nhwd/dot_general | solution.py:63
  2.5 27.9 %all-gather.3 = f32[8,2,256]{2,1,0:T(2,128)S(1)} all-gather(f32[1,2,256]{2,1,0:T(2,128)S(1)} %maximum_bitcast_fusion.2), channel_id=2, replica_groups=mesh['grp'=4,'bn'=8] {'bn'}, dimensions={0}, use_global_device_ids=true | all-gather | bytes 18432 | tf_op jit(solution)/shard_map/all_gather | solution.py:27
  30.5 0.0 copy-done.6
  30.5 0.0 copy-done.8
  30.5 0.2 maximum_convert_fusion.2
  30.7 3.4 %collective-permute-start = (bf16[4,1,64,256]{3,2,1,0:T(8,128)(2,1)S(1)}, bf16[4,1,64,256]{3,2,1,0:T(8,128)(2,1)S(1)}, u32[]{:S(2)}, u32[]{:S(2)}) collective-permute-start(bf16[4,1,64,256]{3,2,1,0:T(8,128)(2,1)S(1)} %get-tuple-element.11), channel_id=1, source_target_pairs={{0,1},{1,2},{2,3},{3,4},{4,5},{5,6},{6,7},{8,9},{9,10},{10,11},{11... | collective-permute-start | bytes 393224 | tf_op jit(solution)/shard_map/ppermute | solution.py:17
  34.2 1.3 %collective-permute-start.1 = (bf16[4,1,64,256]{3,2,1,0:T(8,128)(2,1)S(1)}, bf16[4,1,64,256]{3,2,1,0:T(8,128)(2,1)S(1)}, u32[]{:S(2)}, u32[]{:S(2)}) collective-permute-start(bf16[4,1,64,256]{3,2,1,0:T(8,128)(2,1)S(1)} %get-tuple-element.12), channel_id=1, source_target_pairs={{1,0},{2,1},{3,2},{4,3},{5,4},{6,5},{7,6},{9,8},{10,9},{11,10},{12... | collective-permute-start | bytes 393224 | tf_op jit(solution)/shard_map/ppermute | solution.py:19
  35.5 1.2 %collective-permute-done = bf16[4,1,64,256]{3,2,1,0:T(8,128)(2,1)S(1)} collective-permute-done((bf16[4,1,64,256]{3,2,1,0:T(8,128)(2,1)S(1)}, bf16[4,1,64,256]{3,2,1,0:T(8,128)(2,1)S(1)}, u32[]{:S(2)}, u32[]{:S(2)}) %collective-permute-start) | collective-permute-done | bytes 131104 | tf_op jit(solution)/shard_map/ppermute | solution.py:17
  36.7 4.4 %collective-permute-done.1 = bf16[4,1,64,256]{3,2,1,0:T(8,128)(2,1)S(1)} collective-permute-done((bf16[4,1,64,256]{3,2,1,0:T(8,128)(2,1)S(1)}, bf16[4,1,64,256]{3,2,1,0:T(8,128)(2,1)S(1)}, u32[]{:S(2)}, u32[]{:S(2)}) %collective-permute-start.1) | collective-permute-done | bytes 131104 | tf_op jit(solution)/shard_map/ppermute | solution.py:19
  41.0 0.1 maximum_bitcast_fusion
  41.1 0.6 copy.23
  41.7 0.3 pad.clone
  42.1 0.0 copy-start.9
  42.1 0.1 slice.38
  42.2 0.5 fusion.1
  42.6 0.0 copy-done
  42.6 0.1 copy-done.9
  42.8 0.0 copy-start.7
  42.8 0.0 copy-start.5
  42.8 1.6 %select_reduce_fusion.1 = (f32[256]{0:T(256)S(1)}, f32[256]{0:T(256)S(1)}, f32[4,32,9,256]{3,1,2,0:T(8,128)S(1)}) fusion(pred[32,9]{0,1:T(8,128)(4,1)S(1)} %copy-done.9, bf16[3,3,256,256]{3,2,1,0:T(8,128)(2,1)S(1)} %copy-done, bf16[6,4,8,11,256]{4,1,3,2,0:T(4,128)(2,1)S(1)} %fusion.1), kind=kOutput, calls=%fused_computation.7 | convolution fusion | flops 1360723456 | bytes 3442976 | tf_op jit(solution)/shard_map/conv_general_dilated | solution.py:68
  44.4 26.1 %all-gather.4 = f32[8,2,256]{2,1,0:T(2,128)S(1)} all-gather(f32[1,2,256]{2,1,0:T(2,128)S(1)} %maximum_bitcast_fusion.3), channel_id=3, replica_groups=mesh['grp'=4,'bn'=8] {'bn'}, dimensions={0}, use_global_device_ids=true | all-gather | bytes 18432 | tf_op jit(solution)/shard_map/all_gather | solution.py:27
  70.5 0.0 copy-done.7
  70.5 0.0 copy-done.5
  70.6 0.2 maximum_convert_fusion.1
  70.8 0.0 copy-start.2
  70.8 0.5 copy.18
  71.2 0.2 slice.41
  71.4 0.4 copy-done.2
  71.8 0.0 copy-start.4
  71.8 0.0 copy-start.1
  71.8 0.0 copy-start.3
  71.8 2.6 %fusion.8 = (f32[1024]{0:T(1024)S(1)}, f32[1024]{0:T(1024)S(1)}, f32[4,4,64,1024]{3,2,1,0:T(8,128)}) fusion(bf16[256,1024]{1,0:T(8,128)(2,1)S(1)} %copy-done.2, bf16[4,4,64,256]{3,0,2,1:T(4,128)(2,1)S(1)} %slice.41), kind=kOutput, calls=%fused_computation.31 | convolution fusion | flops 540014592 | bytes 5251072 | tf_op jit(solution)/shard_map/nhwc,cd->nhwd/dot_general | solution.py:79
  74.5 30.5 %all-gather.5 = f32[8,2,1024]{2,1,0:T(2,128)S(1)} all-gather(f32[1,2,1024]{2,1,0:T(2,128)S(1)} %maximum_bitcast_fusion.1), channel_id=4, replica_groups=mesh['grp'=4,'bn'=8] {'bn'}, dimensions={0}, use_global_device_ids=true | all-gather | bytes 73728 | tf_op jit(solution)/shard_map/all_gather | solution.py:27
  105.1 0.0 copy-done.4
  105.1 0.0 copy-done.1
  105.1 0.0 copy-done.3
  105.1 4.5 %maximum_convert_fusion = bf16[4,4,64,1024]{3,2,1,0:T(8,128)(2,1)} fusion(bf16[4,4,64,1024]{3,2,1,0:T(8,128)(2,1)S(1)} %copy-done.1, f32[4,4,64,1024]{3,2,1,0:T(8,128)} %get-tuple-element.21, f32[1024]{0:T(1024)S(1)} %copy-done.3, f32[1024]{0:T(1024)S(1)} %rsqrt_multiply_fusion, f32[1024]{0:T(1024)S(1)} %bitcast.52), kind=kLoop, calls=%fused_computation | loop fusion | flops 7340032 | bytes 8400896 | tf_op jit(solution)/shard_map/convert_element_type | solution.py:81
  (13 shorter events, 0.2 us)
Async XLA Ops:
  0.0 42.6 %copy-start = (bf16[3,3,256,256]{3,2,1,0:T(8,128)(2,1)S(1)}, bf16[3,3,256,256]{3,2,1,0:T(8,128)(2,1)}, u32[]{:S(2)}) copy-start(bf16[3,3,256,256]{3,2,1,0:T(8,128)(2,1)} %param.12) | copy-start | bytes 3538948
  0.0 30.5 %copy-start.6 = (f32[256]{0:T(256)S(1)}, f32[256]{0:T(256)}, u32[]{:S(2)}) copy-start(f32[256]{0:T(256)} %param.14) | copy-start | bytes 3076
  0.0 30.5 %copy-start.8 = (f32[256]{0:T(256)S(1)}, f32[256]{0:T(256)}, u32[]{:S(2)}) copy-start(f32[256]{0:T(256)} %param.15) | copy-start | bytes 3076
  30.7 5.9 %collective-permute-start = (bf16[4,1,64,256]{3,2,1,0:T(8,128)(2,1)S(1)}, bf16[4,1,64,256]{3,2,1,0:T(8,128)(2,1)S(1)}, u32[]{:S(2)}, u32[]{:S(2)}) collective-permute-start(bf16[4,1,64,256]{3,2,1,0:T(8,128)(2,1)S(1)} %get-tuple-element.11), channel_id=1, source_target_pairs={{0,1},{1,2},{2,3},{3,4},{4,5},{5,6},{6,7},{8,9},{9,10},{10,11},{11... | collective-permute-start | bytes 393224 | tf_op jit(solution)/shard_map/ppermute | solution.py:17
  34.2 6.9 %collective-permute-start.1 = (bf16[4,1,64,256]{3,2,1,0:T(8,128)(2,1)S(1)}, bf16[4,1,64,256]{3,2,1,0:T(8,128)(2,1)S(1)}, u32[]{:S(2)}, u32[]{:S(2)}) collective-permute-start(bf16[4,1,64,256]{3,2,1,0:T(8,128)(2,1)S(1)} %get-tuple-element.12), channel_id=1, source_target_pairs={{1,0},{2,1},{3,2},{4,3},{5,4},{6,5},{7,6},{9,8},{10,9},{11,10},{12... | collective-permute-start | bytes 393224 | tf_op jit(solution)/shard_map/ppermute | solution.py:19
  42.1 0.7 copy-start.9
  42.8 27.8 %copy-start.7 = (f32[256]{0:T(256)S(1)}, f32[256]{0:T(256)}, u32[]{:S(2)}) copy-start(f32[256]{0:T(256)} %param.16) | copy-start | bytes 3076
  42.8 27.8 %copy-start.5 = (f32[256]{0:T(256)S(1)}, f32[256]{0:T(256)}, u32[]{:S(2)}) copy-start(f32[256]{0:T(256)} %param.17) | copy-start | bytes 3076
  70.8 1.0 copy-start.2
  71.8 33.3 %copy-start.4 = (f32[1024]{0:T(1024)S(1)}, f32[1024]{0:T(1024)}, u32[]{:S(2)}) copy-start(f32[1024]{0:T(1024)} %param.18) | copy-start | bytes 12292
  71.8 33.3 %copy-start.1 = (bf16[4,4,64,1024]{3,2,1,0:T(8,128)(2,1)S(1)}, bf16[4,4,64,1024]{3,2,1,0:T(8,128)(2,1)}, u32[]{:S(2)}) copy-start(bf16[4,4,64,1024]{3,2,1,0:T(8,128)(2,1)} %param.10) | copy-start | bytes 6291460
  71.8 33.3 %copy-start.3 = (f32[1024]{0:T(1024)S(1)}, f32[1024]{0:T(1024)}, u32[]{:S(2)}) copy-start(f32[1024]{0:T(1024)} %param.19) | copy-start | bytes 12292
where the time goes:
time: 110 us
  blocking collectives  84.6 us (77%)
  matrix products  6.72 us (6%)
  waiting for transfers between devices  5.56 us (5%)
  other arithmetic  5.54 us (5%)
  starting transfers between devices  4.73 us (4%)
  local copies, waits for them, and re-layouts  2.2 us (2%)
    all_gather x3, blocking collectives, group_sum(): gathered = lax.all_gather(partial_value[None], 'bn', axis=0, tiled=True)  84.6 us
    convert_element_type x1, other arithmetic, body(): return jax.nn.relu(summed).astype(jnp.bfloat16)  4.47 us
    ppermute x1, waiting for transfers between devices, padded_2(): lax.ppermute(head, axis, [((i + 1) % count, i) for i in range(ends)])  4.36 us
    ppermute x1, starting transfers between devices, padded_2(): lax.ppermute(tail, axis, [(i, (i + 1) % count) for i in range(ends)])  3.44 us
    dot_general x1, matrix products, body(): jnp.einsum('nhwc,cd->nhwd', hidden_middle, w_expand, preferred_element_ty...  2.64 us
    dot_general x1, matrix products, body(): jnp.einsum('nhwc,cd->nhwd', images, w_reduce, preferred_element_type=jnp....  2.49 us
  transfers between devices with their start and end apart: 2, of which 2 were waited for; matrix products, arithmetic and copies ran while one was open for 0% of the time, Pallas kernels for 0%

commit v1 on v0

v1 whole, which is shorter than its diff:
```python
import functools

import jax
import jax.numpy as jnp
from jax import lax
from jax.experimental import pallas as pl
from jax.experimental.pallas import tpu as pltpu
from jax.sharding import PartitionSpec as P

epsilon = 1e-05
AXIS = "bn"
f32 = jnp.float32
bf16 = jnp.bfloat16
PIVOT_ROWS = 16


def dot(a, b):
    return jnp.dot(a, b, preferred_element_type=f32)


def kernel(
    n, imgs, rows, wid,
    images, w_reduce, w_spatial, w_expand, g1, b1, g2, b2, g3,
    h_out, coef,
    xbuf, wr, ws, we, g1v, b1v, g2v, b2v, g3v,
    first, xcat, middle, hm, up_src, down_src, up_dst, down_dst,
    st1, st2, st3,
    load_sem, out_sem, halo_send, halo_recv, st_send, st_recv,
):
    me = lax.axis_index(AXIS)
    cells = imgs * wid
    count = rows * cells
    mid = wr.shape[1]

    barrier = pltpu.get_barrier_semaphore()
    for k in range(1, n):
        pl.semaphore_signal(
            barrier, inc=1, device_id={AXIS: lax.rem(me + k, n)},
            device_id_type=pl.DeviceIdType.MESH,
        )

    edges = [0] + ([rows - 1] if rows > 1 else [])
    order = edges + [r for r in range(rows) if r not in edges]
    slot = iter(range(load_sem.shape[0]))

    def load(src, dst):
        copy = pltpu.make_async_copy(src, dst, load_sem.at[next(slot)])
        copy.start()
        return copy

    wr_copy = load(w_reduce, wr)
    x_copies = {r: load(images.at[:, r], xbuf.at[r]) for r in order}
    first_vec = [load(g1, g1v), load(b1, b1v)]
    ws_copy = load(w_spatial, ws)
    mid_vec = [load(g2, g2v), load(b2, b2v)]
    we_copy = load(w_expand, we)
    last_vec = [load(g3, g3v)]

    has_up = me > 0
    has_down = me < n - 1
    up_copy = pltpu.make_async_remote_copy(
        src_ref=up_src, dst_ref=up_dst, send_sem=halo_send.at[0], recv_sem=halo_recv.at[0],
        device_id={AXIS: lax.rem(me + n - 1, n)}, device_id_type=pl.DeviceIdType.MESH,
    )
    down_copy = pltpu.make_async_remote_copy(
        src_ref=down_src, dst_ref=down_dst, send_sem=halo_send.at[1], recv_sem=halo_recv.at[1],
        device_id={AXIS: lax.rem(me + 1, n)}, device_id_type=pl.DeviceIdType.MESH,
    )

    def exchange_start(index, buf):
        copies = []
        for k in range(1, n):
            copy = pltpu.make_async_remote_copy(
                src_ref=buf.at[0], dst_ref=buf.at[k],
                send_sem=st_send.at[index, k - 1], recv_sem=st_recv.at[index, k - 1],
                device_id={AXIS: lax.rem(me + k, n)}, device_id_type=pl.DeviceIdType.MESH,
            )
            copy.start()
            copies.append(copy)
        return copies

    def exchange_end(copies, buf):
        for copy in copies:
            copy.wait_recv()
        values = buf[...]
        total = jnp.sum(values, axis=0)
        average = total[0:1] / n
        gap = values[:, 0:1, :] - average
        spread = (total[1:2] + count * jnp.sum(gap * gap, axis=0)) / (n * count)
        return average, spread

    wr_copy.wait()
    total = jnp.zeros((1, mid), f32)
    for r in order:
        x_copies[r].wait()
        value = dot(xbuf[r].reshape(cells, xbuf.shape[-1]), wr[...])
        first[r] = value
        part = jnp.sum(value, axis=0, keepdims=True)
        total = total + part
        for row, src in ((0, up_src), (rows - 1, down_src)):
            if r == row:
                pivot = (part / cells).astype(bf16)
                src[pl.ds(0, cells), :] = (value - pivot.astype(f32)).astype(bf16)
                src[pl.ds(cells, PIVOT_ROWS), :] = jnp.broadcast_to(pivot, (PIVOT_ROWS, mid))
    average = total / count
    second = jnp.zeros((1, mid), f32)
    for r in range(rows):
        gap = first[r] - average
        second = second + jnp.sum(gap * gap, axis=0, keepdims=True)
    st1[0, 0:1, :] = average
    st1[0, 1:2, :] = second

    pl.semaphore_wait(barrier, n - 1)
    copies1 = exchange_start(0, st1)

    @pl.when(has_up)
    def _():
        up_copy.start()

    @pl.when(has_down)
    def _():
        down_copy.start()

    for copy in first_vec:
        copy.wait()
    average, spread = exchange_end(copies1, st1)
    scale = g1v[...] * lax.rsqrt(spread + epsilon)
    shift = b1v[...]
    column = lax.rem(lax.broadcasted_iota(jnp.int32, (cells, mid), 0), wid)

    def fill(r, value):
        h = jnp.maximum((value - average) * scale + shift, 0.0)
        xcat[r, :, pl.ds(mid, mid)] = h.astype(bf16)
        before = jnp.where(column == 0, 0.0, pltpu.roll(h, 1, 0))
        xcat[r, :, pl.ds(0, mid)] = before.astype(bf16)
        after = jnp.where(column == wid - 1, 0.0, pltpu.roll(h, cells - 1, 0))
        xcat[r, :, pl.ds(2 * mid, mid)] = after.astype(bf16)

    for r in range(rows):
        fill(r + 1, first[r])

    ws_copy.wait()
    for r in range(rows):
        acc = dot(xcat[r + 1], ws[1])
        if r > 0:
            acc = acc + dot(xcat[r], ws[0])
        if r < rows - 1:
            acc = acc + dot(xcat[r + 2], ws[2])
        middle[r] = acc

    def halo(src):
        return src[pl.ds(0, cells), :].astype(f32) + src[pl.ds(cells, 1), :].astype(f32)

    @pl.when(has_up)
    def _():
        down_copy.wait_recv()
        fill(0, halo(down_dst))
        middle[0] += dot(xcat[0], ws[0])

    @pl.when(has_down)
    def _():
        up_copy.wait_recv()
        fill(rows + 1, halo(up_dst))
        middle[rows - 1] += dot(xcat[rows + 1], ws[2])

    total = jnp.zeros((1, mid), f32)
    for r in range(rows):
        total = total + jnp.sum(middle[r], axis=0, keepdims=True)
    average = total / count
    second = jnp.zeros((1, mid), f32)
    for r in range(rows):
        gap = middle[r] - average
        second = second + jnp.sum(gap * gap, axis=0, keepdims=True)
    st2[0, 0:1, :] = average
    st2[0, 1:2, :] = second
    copies2 = exchange_start(1, st2)
    for copy in mid_vec + last_vec:
        copy.wait()
    we_copy.wait()
    average, spread = exchange_end(copies2, st2)
    scale = g2v[...] * lax.rsqrt(spread + epsilon)
    shift = b2v[...]
    out_copies = []
    total = jnp.zeros((1, mid), f32)
    for r in range(rows):
        h = jnp.maximum((middle[r] - average) * scale + shift, 0.0)
        total = total + jnp.sum(h, axis=0, keepdims=True)
        hm[r] = h.astype(bf16).reshape(imgs, wid, mid)
        copy = pltpu.make_async_copy(hm.at[r], h_out.at[:, r], out_sem.at[r])
        copy.start()
        out_copies.append(copy)

    pivot = dot((total / count).astype(bf16), we[...])
    one = jnp.zeros_like(pivot)
    two = jnp.zeros_like(pivot)
    for r in range(rows):
        gap = dot(hm[r].reshape(cells, mid), we[...]) - pivot
        one = one + jnp.sum(gap, axis=0, keepdims=True)
        two = two + jnp.sum(gap * gap, axis=0, keepdims=True)
    st3[0, 0:1, :] = pivot + one / count
    st3[0, 1:2, :] = two - one * (one / count)
    copies3 = exchange_start(2, st3)
    for copy in copies1 + copies2:
        copy.wait_send()

    @pl.when(has_up)
    def _():
        up_copy.wait_send()

    @pl.when(has_down)
    def _():
        down_copy.wait_send()

    for copy in out_copies:
        copy.wait()
    average, spread = exchange_end(copies3, st3)
    coef[0:1, :] = average
    coef[1:2, :] = g3v[...] * lax.rsqrt(spread + epsilon)
    for copy in copies3:
        copy.wait_send()


def body(images, w_reduce, w_spatial, w_expand, g1, b1, g2, b2, g3, b3):
    n = lax.axis_size(AXIS)
    imgs, rows, wid, ch = images.shape
    mid = w_reduce.shape[1]
    cells = imgs * wid
    any_spec = pl.BlockSpec(memory_space=pl.ANY)
    vec = lambda c: pltpu.VMEM((1, c), f32)
    rowvec = lambda v: v.reshape(1, v.shape[0])
    halo = pltpu.VMEM((cells + PIVOT_ROWS, mid), bf16)
    hidden, coef = pl.pallas_call(
        functools.partial(kernel, n, imgs, rows, wid),
        out_shape=(
            jax.ShapeDtypeStruct((imgs, rows, wid, mid), bf16),
            jax.ShapeDtypeStruct((2, ch), f32),
        ),
        in_specs=[any_spec] * 9,
        out_specs=(any_spec, pl.BlockSpec(memory_space=pltpu.VMEM)),
        scratch_shapes=[
            pltpu.VMEM((rows, imgs, wid, ch), bf16),
            pltpu.VMEM((ch, mid), bf16),
            pltpu.VMEM((3, 3 * mid, mid), bf16),
            pltpu.VMEM((mid, ch), bf16),
            vec(mid), vec(mid), vec(mid), vec(mid), vec(ch),
            pltpu.VMEM((rows, cells, mid), f32),
            pltpu.VMEM((rows + 2, cells, 3 * mid), bf16),
            pltpu.VMEM((rows, cells, mid), f32),
            pltpu.VMEM((rows, imgs, wid, mid), bf16),
            halo, halo, halo, halo,
            pltpu.VMEM((n, 2, mid), f32),
            pltpu.VMEM((n, 2, mid), f32),
            pltpu.VMEM((n, 2, ch), f32),
            pltpu.SemaphoreType.DMA((rows + 8,)),
            pltpu.SemaphoreType.DMA((rows,)),
            pltpu.SemaphoreType.DMA((2,)),
            pltpu.SemaphoreType.DMA((2,)),
            pltpu.SemaphoreType.DMA((3, n - 1)),
            pltpu.SemaphoreType.DMA((3, n - 1)),
        ],
        compiler_params=pltpu.CompilerParams(
            collective_id=0, has_side_effects=True, vmem_limit_bytes=32 * 1024 * 1024
        ),
        name="block_front",
    )(
        images, w_reduce, w_spatial.reshape(3, 3 * mid, mid), w_expand,
        rowvec(g1), rowvec(b1), rowvec(g2), rowvec(b2), rowvec(g3),
    )
    last = jnp.einsum("nhwc,cd->nhwd", hidden, w_expand, preferred_element_type=f32)
    summed = (last - coef[0]) * coef[1] + b3 + images.astype(f32)
    return jax.nn.relu(summed).astype(bf16)


def solution(mesh):
    placed = (P("grp", "bn", None, None), P(), P(), P(), P(), P(), P(), P(), P(), P())
    return jax.shard_map(
        body, mesh=mesh, in_specs=placed, out_specs=P("grp", "bn", None, None), check_vma=False
    )
```

time: 110 us -> 35.1 us (0.32)
  blocking collectives: 84.6 us -> 0 us
  Pallas kernels: 0 us -> 23.9 us
  local copies, waits for them, and re-layouts: 2.2 us -> 8.35 us
  waiting for transfers between devices: 5.56 us -> 0 us
  other arithmetic: 5.54 us -> 0 us
  starting transfers between devices: 4.73 us -> 0 us
  matrix products: 6.72 us -> 2.45 us
    all_gather x3 -> x0, blocking collectives: 84.6 us -> none  [group_sum(): gathered = lax.all_gather(partial_value[None], 'bn', axis=0, tiled=True)]
    pallas_call x0 -> x1, Pallas kernels: none -> 23.9 us  [body(): pl.pallas_call(functools.partial(kernel, n, imgs, rows, wid), out_shape=(...]
    unnamed x21 -> x20, local copies, waits for them, and re-layouts: 1.15 us -> 8.35 us
    ppermute x2 -> x0, waiting for transfers between devices: 5.56 us -> none  [the longest x1 4.36 us: padded_2(): lax.ppermute(head, axis, [((i + 1) % count, i) for i in range(ends)])]
    convert_element_type x3 -> x0, other arithmetic: 4.83 us -> none  [the longest x1 4.47 us: body(): return jax.nn.relu(summed).astype(jnp.bfloat16)]
    ppermute x2 -> x0, starting transfers between devices: 4.73 us -> none  [the longest x1 3.44 us: padded_2(): lax.ppermute(tail, axis, [(i, (i + 1) % count) for i in range(ends)])]
    dot_general x2 -> x1, matrix products: 5.14 us -> 2.45 us  [body(): jnp.einsum('nhwc,cd->nhwd', hidden, w_expand, preferred_element_type=f32)]
    conv_general_dilated x1 -> x0, matrix products: 1.58 us -> none  [body(): lax.conv_general_dilated(padded, w_spatial, (1, 1), ((0, 0), (1, 1)), dim...]
  transfers between devices with their start and end apart: 2 -> 0, of which waited for: 2 -> 0; matrix products, arithmetic and copies ran while one was open for 0% -> 0% of each run, Pallas kernels for 0% -> 0%
where the time goes in v1:
time: 35.1 us; the launch traced here: 34.7 us
  Pallas kernels  23.9 us (68%)
  local copies, waits for them, and re-layouts  8.35 us (24%)
  matrix products  2.45 us (7%)
    pallas_call x1, Pallas kernels, body(): pl.pallas_call(functools.partial(kernel, n, imgs, rows, wid), out_shape=(...  23.9 us
    unnamed x20, local copies, waits for them, and re-layouts  8.35 us
    dot_general x1, matrix products, body(): jnp.einsum('nhwc,cd->nhwd', hidden, w_expand, preferred_element_type=f32)  2.45 us

profile of v1, /device:TPU:0, one launch (start us, length us, event | category | flops | bytes accessed | tf_op | source)
XLA Modules:
  0.0 34.7 jit_solution(499487740127183362)
XLA Ops:
  0.0 0.0 copy-start
  0.0 1.6 %copy-done = bf16[4,4,64,1024]{3,2,1,0:T(8,128)(2,1)S(1)} copy-done((bf16[4,4,64,1024]{3,2,1,0:T(8,128)(2,1)S(1)}, bf16[4,4,64,1024]{3,2,1,0:T(8,128)(2,1)}, u32[]{:S(2)}) %copy-start) | copy-done | bytes 2097176
  1.6 0.0 copy-start.1
  1.6 1.3 %copy-done.1 = bf16[3,3,256,256]{3,2,1,0:T(8,128)(2,1)S(1)} copy-done((bf16[3,3,256,256]{3,2,1,0:T(8,128)(2,1)S(1)}, bf16[3,3,256,256]{3,2,1,0:T(8,128)(2,1)}, u32[]{:S(2)}) %copy-start.1) | copy-done | bytes 1179672
  2.9 0.0 copy-start.2
  2.9 1.0 %copy-done.2 = bf16[1024,256]{1,0:T(8,128)(2,1)S(1)} copy-done((bf16[1024,256]{1,0:T(8,128)(2,1)S(1)}, bf16[1024,256]{1,0:T(8,128)(2,1)}, u32[]{:S(2)}) %copy-start.2) | copy-done | bytes 524312
  3.9 0.0 copy-start.3
  3.9 1.0 %copy-done.3 = bf16[256,1024]{1,0:T(8,128)(2,1)S(1)} copy-done((bf16[256,1024]{1,0:T(8,128)(2,1)S(1)}, bf16[256,1024]{1,0:T(8,128)(2,1)}, u32[]{:S(2)}) %copy-start.3) | copy-done | bytes 524312
  4.9 0.0 copy-start.4
  4.9 0.7 %copy-done.4 = f32[1024]{0:T(1024)S(1)} copy-done((f32[1024]{0:T(1024)S(1)}, f32[1024]{0:T(1024)}, u32[]{:S(2)}) %copy-start.4) | copy-done | bytes 4120
  5.6 0.0 copy-start.5
  5.6 0.7 %copy-done.5 = f32[256]{0:T(256)S(1)} copy-done((f32[256]{0:T(256)S(1)}, f32[256]{0:T(256)}, u32[]{:S(2)}) %copy-start.5) | copy-done | bytes 1048
  6.3 0.0 copy-start.6
  6.3 0.7 %copy-done.6 = f32[256]{0:T(256)S(1)} copy-done((f32[256]{0:T(256)S(1)}, f32[256]{0:T(256)}, u32[]{:S(2)}) %copy-start.6) | copy-done | bytes 1048
  7.0 0.0 copy-start.7
  7.0 0.7 %copy-done.7 = f32[256]{0:T(256)S(1)} copy-done((f32[256]{0:T(256)S(1)}, f32[256]{0:T(256)}, u32[]{:S(2)}) %copy-start.7) | copy-done | bytes 1048
  7.7 0.0 copy-start.8
  7.7 0.7 %copy-done.8 = f32[256]{0:T(256)S(1)} copy-done((f32[256]{0:T(256)S(1)}, f32[256]{0:T(256)}, u32[]{:S(2)}) %copy-start.8) | copy-done | bytes 1048
  8.4 0.0 copy-start.9
  8.4 23.9 %block_front.1 = (bf16[4,4,64,256]{3,2,1,0:T(8,128)(2,1)S(1)}, f32[2,1024]{1,0:T(2,128)S(1)}) custom-call(bf16[4,4,64,1024]{3,2,1,0:T(8,128)(2,1)S(1)} %copy-done, bf16[1024,256]{1,0:T(8,128)(2,1)S(1)} %copy-done.2, bf16[3,768,256]{2,1,0:T(8,128)(2,1)S(1)} %bitcast.14, bf16[256,1024]{1,0:T(8,128)(2,1)S(1)} %copy-done.3, f32[1,256]{1,0:T(1,128)S(1)} %bitcast.16, ...), custom_call_target="tpu_custom_call" | custom-call | tf_op jit(solution)/shard_map/block_front/pallas_call | solution.py:232
  32.3 0.0 copy-done.9
  32.3 2.4 %maximum_convert_fusion = bf16[4,4,64,1024]{3,2,1,0:T(8,128)(2,1)} fusion(bf16[4,4,64,1024]{3,2,1,0:T(8,128)(2,1)S(1)} %copy-done, bf16[4,4,64,256]{3,2,1,0:T(8,128)(2,1)S(1)} %get-tuple-element.7, f32[1024]{0:T(1024)S(1)} %copy-done.9, f32[1024]{0:T(1024)S(1)} %bitcast.21, f32[1024]{0:T(1024)S(1)} %bitcast.20, bf16[256,1024]{1,0:T(8,128)(2,1)S(1)} %copy-done.3), kind=kOutput, calls=%fused_computation | convolution fusion | flops 544210944 | bytes 5255168 | tf_op jit(solution)/shard_map/nhwc,cd->nhwd/dot_general | solution.py:269
  (1 shorter events, 0.0 us)
Async XLA Ops:
  0.0 1.6 %copy-start = (bf16[4,4,64,1024]{3,2,1,0:T(8,128)(2,1)S(1)}, bf16[4,4,64,1024]{3,2,1,0:T(8,128)(2,1)}, u32[]{:S(2)}) copy-start(bf16[4,4,64,1024]{3,2,1,0:T(8,128)(2,1)} %images.1) | copy-start | bytes 6291460
  1.6 1.3 %copy-start.1 = (bf16[3,3,256,256]{3,2,1,0:T(8,128)(2,1)S(1)}, bf16[3,3,256,256]{3,2,1,0:T(8,128)(2,1)}, u32[]{:S(2)}) copy-start(bf16[3,3,256,256]{3,2,1,0:T(8,128)(2,1)} %param.12) | copy-start | bytes 3538948
  2.9 1.0 %copy-start.2 = (bf16[1024,256]{1,0:T(8,128)(2,1)S(1)}, bf16[1024,256]{1,0:T(8,128)(2,1)}, u32[]{:S(2)}) copy-start(bf16[1024,256]{1,0:T(8,128)(2,1)} %w_reduce.1) | copy-start | bytes 1572868
  3.9 1.0 %copy-start.3 = (bf16[256,1024]{1,0:T(8,128)(2,1)S(1)}, bf16[256,1024]{1,0:T(8,128)(2,1)}, u32[]{:S(2)}) copy-start(bf16[256,1024]{1,0:T(8,128)(2,1)} %w_expand.1) | copy-start | bytes 1572868
  4.9 0.7 %copy-start.4 = (f32[1024]{0:T(1024)S(1)}, f32[1024]{0:T(1024)}, u32[]{:S(2)}) copy-start(f32[1024]{0:T(1024)} %param.18) | copy-start | bytes 12292
  5.6 0.7 %copy-start.5 = (f32[256]{0:T(256)S(1)}, f32[256]{0:T(256)}, u32[]{:S(2)}) copy-start(f32[256]{0:T(256)} %param.14) | copy-start | bytes 3076
  6.3 0.7 %copy-start.6 = (f32[256]{0:T(256)S(1)}, f32[256]{0:T(256)}, u32[]{:S(2)}) copy-start(f32[256]{0:T(256)} %param.15) | copy-start | bytes 3076
  7.0 0.7 %copy-start.7 = (f32[256]{0:T(256)S(1)}, f32[256]{0:T(256)}, u32[]{:S(2)}) copy-start(f32[256]{0:T(256)} %param.16) | copy-start | bytes 3076
  7.7 0.7 %copy-start.8 = (f32[256]{0:T(256)S(1)}, f32[256]{0:T(256)}, u32[]{:S(2)}) copy-start(f32[256]{0:T(256)} %param.17) | copy-start | bytes 3076
  8.4 23.9 %copy-start.9 = (f32[1024]{0:T(1024)S(1)}, f32[1024]{0:T(1024)}, u32[]{:S(2)}) copy-start(f32[1024]{0:T(1024)} %param.19) | copy-start | bytes 12292

commit v2 on v1

v2 whole, which is shorter than its diff:
```python
import functools

import jax
import jax.numpy as jnp
from jax import lax
from jax.experimental import pallas as pl
from jax.experimental.pallas import tpu as pltpu
from jax.sharding import PartitionSpec as P

epsilon = 1e-05
AXIS = "bn"
f32 = jnp.float32
bf16 = jnp.bfloat16
PIVOT_ROWS = 16
PIECES = 8


def dot(a, b):
    return jnp.dot(a, b, preferred_element_type=f32)


def flipped(me, k):
    bit, out = 1, me
    while bit <= k:
        if k & bit:
            out = out + bit * (1 - 2 * lax.rem(me // bit, 2))
        bit *= 2
    return out


def kernel(
    n, imgs, rows, wid, chunks,
    images, w_reduce, w_spatial, w_expand, g1, b1, g2, b2, g3,
    x_out, last_out, coef,
    wr, ws, we, g1v, b1v, g2v, b2v, g3v,
    first, xcat, middle, up_src, down_src, up_dst, down_dst,
    st1, st2, st3,
    load_sem, halo_send, halo_recv, st_send, st_recv,
):
    me = lax.axis_index(AXIS)
    cells = imgs * wid
    sizes = [c * wid for c in chunks]
    starts = [sum(sizes[:c]) for c in range(len(sizes))]
    chunks = len(sizes)
    count = rows * cells
    mid = wr.shape[1]
    ch = wr.shape[0]
    paired = n & (n - 1) == 0

    def peer(k):
        return flipped(me, k) if paired else lax.rem(me + k, n)

    hops = list(range(n - 1, 0, -1))
    barrier = pltpu.get_barrier_semaphore()
    for k in hops:
        pl.semaphore_signal(
            barrier, inc=1, device_id={AXIS: peer(k)}, device_id_type=pl.DeviceIdType.MESH
        )

    edges = [0] + ([rows - 1] if rows > 1 else [])
    inner = [r for r in range(rows) if r not in edges]
    slot = iter(range(load_sem.shape[0]))

    def load(src, dst):
        copy = pltpu.make_async_copy(src, dst, load_sem.at[next(slot)])
        copy.start()
        return copy

    wr_copy = load(w_reduce, wr)
    x_copies = {r: load(images.at[:, r], x_out.at[:, r]) for r in edges + inner}
    first_vec = [load(g1, g1v), load(b1, b1v)]
    ws_copy = load(w_spatial, ws)
    mid_vec = [load(g2, g2v), load(b2, b2v)]
    we_copy = load(w_expand, we)
    last_vec = [load(g3, g3v)]

    has_up = me > 0
    has_down = me < n - 1

    def span(c):
        begin = 0 if c == 0 else PIVOT_ROWS + starts[c]
        return pl.ds(begin, PIVOT_ROWS + starts[c] + sizes[c] - begin)

    def halo_copy(c, side):
        src, dst, to = ((up_src, up_dst, n - 1), (down_src, down_dst, 1))[side]
        return pltpu.make_async_remote_copy(
            src_ref=src.at[span(c)], dst_ref=dst.at[span(c)],
            send_sem=halo_send.at[side, c], recv_sem=halo_recv.at[side, c],
            device_id={AXIS: lax.rem(me + to, n)}, device_id_type=pl.DeviceIdType.MESH,
        )

    up_copies = [halo_copy(c, 0) for c in range(chunks)]
    down_copies = [halo_copy(c, 1) for c in range(chunks)]

    def exchange_start(index, buf):
        copies = []
        for k in hops:
            copy = pltpu.make_async_remote_copy(
                src_ref=buf.at[0], dst_ref=buf.at[k],
                send_sem=st_send.at[index, k - 1], recv_sem=st_recv.at[index, k - 1],
                device_id={AXIS: peer(k)}, device_id_type=pl.DeviceIdType.MESH,
            )
            copy.start()
            copies.append(copy)
        return copies

    def exchange_end(copies, buf):
        for copy in copies:
            copy.wait_recv()
        values = buf[...]
        total = jnp.sum(values, axis=0)
        average = total[0:1] / n
        gap = values[:, 0:1, :] - average
        spread = (total[1:2] + count * jnp.sum(gap * gap, axis=0)) / (n * count)
        return average, spread

    def colsum(v):
        return jnp.sum(v, axis=0, keepdims=True)

    def pooled(buf, pivot, one, two):
        buf[0, 0:1, :] = pivot + one / count
        buf[0, 1:2, :] = two - one * (one / count)

    wr_copy.wait()
    pivot = None
    one = jnp.zeros((1, mid), f32)
    two = jnp.zeros((1, mid), f32)
    for r in edges + inner:
        x_copies[r].wait()
        value = dot(x_out[:, r].reshape(cells, ch), wr[...])
        first[r] = value
        if pivot is None:
            pivot = colsum(value) / cells
        gap = value - pivot
        one = one + colsum(gap)
        two = two + colsum(gap * gap)
        for row, src in ((0, up_src), (rows - 1, down_src)):
            if r == row:
                centre = (colsum(value) / cells).astype(bf16)
                sent = (value - centre.astype(f32)).astype(bf16)
                src[pl.ds(0, PIVOT_ROWS), :] = jnp.broadcast_to(centre, (PIVOT_ROWS, mid))
                src[pl.ds(PIVOT_ROWS, cells), :] = sent
    pooled(st1, pivot, one, two)

    pl.semaphore_wait(barrier, n - 1)
    copies1 = exchange_start(0, st1)
    for c in range(chunks):
        pl.when(has_up)(up_copies[c].start)
        pl.when(has_down)(down_copies[c].start)

    for copy in first_vec:
        copy.wait()
    average, spread = exchange_end(copies1, st1)
    scale = g1v[...] * lax.rsqrt(spread + epsilon)
    shift = b1v[...]

    def columns(size):
        shape = (size // wid, wid, mid)
        return lax.broadcasted_iota(jnp.int32, shape, 1).reshape(size, mid)

    def fill(r, start, value):
        size = value.shape[0]
        column = columns(size)
        h = jnp.maximum((value - average) * scale + shift, 0.0)
        here = pl.ds(start, size)
        xcat[r, here, pl.ds(mid, mid)] = h.astype(bf16)
        before = jnp.where(column == 0, 0.0, pltpu.roll(h, 1, 0))
        xcat[r, here, pl.ds(0, mid)] = before.astype(bf16)
        after = jnp.where(column == wid - 1, 0.0, pltpu.roll(h, size - 1, 0))
        xcat[r, here, pl.ds(2 * mid, mid)] = after.astype(bf16)

    for r in range(rows):
        fill(r + 1, 0, first[r])

    ws_copy.wait()
    for r in range(rows):
        acc = dot(xcat[r + 1], ws[1])
        if r > 0:
            acc = acc + dot(xcat[r], ws[0])
        if r < rows - 1:
            acc = acc + dot(xcat[r + 2], ws[2])
        middle[r] = acc

    based = inner or edges
    pivot = jnp.zeros((1, mid), f32)
    for r in based:
        pivot = pivot + colsum(middle[r])
    pivot = pivot / (len(based) * cells)
    one = jnp.zeros((1, mid), f32)
    two = jnp.zeros((1, mid), f32)
    for r in inner:
        gap = middle[r] - pivot
        one = one + colsum(gap)
        two = two + colsum(gap * gap)

    def add_halo(dst, c, padded_row, row, tap):
        value = dst[pl.ds(PIVOT_ROWS + starts[c], sizes[c]), :].astype(f32)
        fill(padded_row, starts[c], value + dst[pl.ds(0, 1), :].astype(f32))
        here = pl.ds(starts[c], sizes[c])
        middle[row, here, :] += dot(xcat[padded_row, here, :], ws[tap])

    for c in range(chunks):
        @pl.when(has_down)
        def _():
            up_copies[c].wait_recv()
            add_halo(up_dst, c, rows + 1, rows - 1, 2)

        @pl.when(has_up)
        def _():
            down_copies[c].wait_recv()
            add_halo(down_dst, c, 0, 0, 0)

        for r in edges:
            gap = middle[r, pl.ds(starts[c], sizes[c]), :] - pivot
            one = one + colsum(gap)
            two = two + colsum(gap * gap)

    pooled(st2, pivot, one, two)
    copies2 = exchange_start(1, st2)
    for copy in mid_vec + last_vec:
        copy.wait()
    we_copy.wait()
    for copy in copies1:
        copy.wait_send()
    for c in range(chunks):
        pl.when(has_up)(up_copies[c].wait_send)
        pl.when(has_down)(down_copies[c].wait_send)
    average, spread = exchange_end(copies2, st2)
    scale = g2v[...] * lax.rsqrt(spread + epsilon)
    shift = b2v[...]

    total = jnp.zeros((1, mid), f32)
    hidden = []
    for r in range(rows):
        h = jnp.maximum((middle[r] - average) * scale + shift, 0.0).astype(bf16)
        total = total + colsum(h.astype(f32))
        hidden.append(h)
    rest = total / count
    pieces = []
    for _ in range(3):
        piece = rest.astype(bf16).astype(f32)
        rest = rest - piece
        pieces.append(piece)
    pieces = jnp.concatenate(pieces + [jnp.zeros((13, mid), f32)], axis=0)
    pivot = colsum(dot(pieces.astype(bf16), we[...]))
    two = jnp.zeros((1, ch), f32)
    for r in range(rows):
        value = dot(hidden[r], we[...])
        last_out[:, r] = value.reshape(imgs, wid, ch)
        gap = value - pivot
        two = two + colsum(gap * gap)
    st3[0, 0:1, :] = pivot
    st3[0, 1:2, :] = two
    copies3 = exchange_start(2, st3)
    for copy in copies2:
        copy.wait_send()
    average, spread = exchange_end(copies3, st3)
    coef[0:1, :] = average
    coef[1:2, :] = g3v[...] * lax.rsqrt(spread + epsilon)
    for copy in copies3:
        copy.wait_send()


def finish(pieces, last, held, coef, b3, out, done, sem):
    rows = last.shape[0] // pieces
    scale = coef[1:2, :]
    mean = coef[0:1, :]
    shift = b3[...]
    copies = []
    for i in range(pieces):
        here = pl.ds(i * rows, rows)
        value = (last[here, :] - mean) * scale + shift + held[here, :].astype(f32)
        done[here, :] = jnp.maximum(value, 0.0).astype(bf16)
        copy = pltpu.make_async_copy(done.at[here], out.at[here], sem.at[i])
        copy.start()
        copies.append(copy)
    for copy in copies:
        copy.wait()


def body(images, w_reduce, w_spatial, w_expand, g1, b1, g2, b2, g3, b3):
    n = lax.axis_size(AXIS)
    imgs, rows, wid, ch = images.shape
    mid = w_reduce.shape[1]
    cells = imgs * wid
    chunks = [imgs // 2, imgs - imgs // 2] if imgs > 1 else [imgs]
    hbm = pl.BlockSpec(memory_space=pltpu.HBM)
    vmem = pl.BlockSpec(memory_space=pltpu.VMEM)
    vec = lambda c: pltpu.VMEM((1, c), f32)
    rowvec = lambda v: v.reshape(1, v.shape[0])
    halo = pltpu.VMEM((cells + PIVOT_ROWS, mid), bf16)
    held, last, coef = pl.pallas_call(
        functools.partial(kernel, n, imgs, rows, wid, chunks),
        out_shape=(
            jax.ShapeDtypeStruct(images.shape, bf16),
            jax.ShapeDtypeStruct(images.shape, f32),
            jax.ShapeDtypeStruct((2, ch), f32),
        ),
        in_specs=[hbm] * 9,
        out_specs=(vmem, vmem, vmem),
        scratch_shapes=[
            pltpu.VMEM((ch, mid), bf16),
            pltpu.VMEM((3, 3 * mid, mid), bf16),
            pltpu.VMEM((mid, ch), bf16),
            vec(mid), vec(mid), vec(mid), vec(mid), vec(ch),
            pltpu.VMEM((rows, cells, mid), f32),
            pltpu.VMEM((rows + 2, cells, 3 * mid), bf16),
            pltpu.VMEM((rows, cells, mid), f32),
            halo, halo, halo, halo,
            pltpu.VMEM((n, 2, mid), f32),
            pltpu.VMEM((n, 2, mid), f32),
            pltpu.VMEM((n, 2, ch), f32),
            pltpu.SemaphoreType.DMA((rows + 8,)),
            pltpu.SemaphoreType.DMA((2, len(chunks))),
            pltpu.SemaphoreType.DMA((2, len(chunks))),
            pltpu.SemaphoreType.DMA((3, n - 1)),
            pltpu.SemaphoreType.DMA((3, n - 1)),
        ],
        compiler_params=pltpu.CompilerParams(
            collective_id=0, has_side_effects=True, vmem_limit_bytes=32 * 1024 * 1024
        ),
        name="block_front",
    )(*[
        pltpu.with_memory_space_constraint(v, pltpu.HBM)
        for v in (
            images, w_reduce, w_spatial.reshape(3, 3 * mid, mid), w_expand,
            rowvec(g1), rowvec(b1), rowvec(g2), rowvec(b2), rowvec(g3),
        )
    ])
    total = imgs * rows * wid
    pieces = PIECES if total % (PIECES * 16) == 0 else 1
    out = pl.pallas_call(
        functools.partial(finish, pieces),
        out_shape=jax.ShapeDtypeStruct((total, ch), bf16),
        in_specs=[vmem] * 4,
        out_specs=hbm,
        scratch_shapes=[pltpu.VMEM((total, ch), bf16), pltpu.SemaphoreType.DMA((pieces,))],
        compiler_params=pltpu.CompilerParams(vmem_limit_bytes=16 * 1024 * 1024),
        name="block_finish",
    )(last.reshape(total, ch), held.reshape(total, ch), coef, rowvec(b3))
    return out.reshape(images.shape)


def solution(mesh):
    placed = (P("grp", "bn", None, None), P(), P(), P(), P(), P(), P(), P(), P(), P())
    return jax.shard_map(
        body, mesh=mesh, in_specs=placed, out_specs=P("grp", "bn", None, None), check_vma=False
    )
```

time: 35.1 us -> 25.7 us (0.73)
  local copies, waits for them, and re-layouts: 8.35 us -> 0.01 us
  matrix products: 2.45 us -> 0 us
  Pallas kernels: 23.9 us -> 25.5 us
    unnamed x20 -> x2, local copies, waits for them, and re-layouts: 8.35 us -> 0.01 us
    dot_general x1 -> x0, matrix products: 2.45 us -> none  [body(): jnp.einsum('nhwc,cd->nhwd', hidden, w_expand, preferred_element_type=f32)]
    pallas_call x1 -> x2, Pallas kernels: 23.9 us -> 25.5 us  [the longest x1 23.9 us: body(): pl.pallas_call(functools.partial(kernel, n, imgs, rows, wid, chunks), out...]
where the time goes in v2:
time: 25.7 us; the launch traced here: 25.6 us
  Pallas kernels  25.5 us (99%)
    pallas_call x1, Pallas kernels, body(): pl.pallas_call(functools.partial(kernel, n, imgs, rows, wid, chunks), out...  23.9 us
    pallas_call x1, Pallas kernels, body(): pl.pallas_call(functools.partial(finish, pieces), out_shape=jax.ShapeDtyp...  1.67 us

profile of v2, /device:TPU:0, one launch (start us, length us, event | category | flops | bytes accessed | tf_op | source)
XLA Modules:
  0.0 25.6 jit_solution(15172582788143828426)
XLA Ops:
  0.0 0.0 copy-start
  0.0 23.9 %block_front.1 = (bf16[4,4,64,1024]{3,2,1,0:T(8,128)(2,1)S(1)}, f32[4,4,64,1024]{3,2,1,0:T(8,128)S(1)}, f32[2,1024]{1,0:T(2,128)S(1)}) custom-call(bf16[4,4,64,1024]{3,2,1,0:T(8,128)(2,1)} %images.1, bf16[1024,256]{1,0:T(8,128)(2,1)} %w_reduce.1, bf16[3,768,256]{2,1,0:T(8,128)(2,1)} %bitcast.13, bf16[256,1024]{1,0:T(8,128)(2,1)} %w_expand.1, ...), custom_call_target="tpu_custom_call" | custom-call | tf_op jit(solution)/shard_map/block_front/pallas_call | solution.py:292
  23.9 0.0 copy-done
  23.9 1.7 %block_finish.1 = bf16[1024,1024]{1,0:T(8,128)(2,1)} custom-call(f32[1024,1024]{1,0:T(8,128)S(1)} %bitcast.10, bf16[1024,1024]{1,0:T(8,128)(2,1)S(1)} %bitcast.11, f32[2,1024]{1,0:T(2,128)S(1)} %get-tuple-element.10.coef, f32[1,1024]{1,0:T(1,128)S(1)} %bitcast.12), custom_call_target="tpu_custom_call" | custom-call | tf_op jit(solution)/shard_map/block_finish/pallas_call | solution.py:332
Async XLA Ops:
  0.0 23.9 %copy-start = (f32[1024]{0:T(1024)S(1)}, f32[1024]{0:T(1024)}, u32[]{:S(2)}) copy-start(f32[1024]{0:T(1024)} %param.19) | copy-start | bytes 12292

commit v3 on v2

--- a/solution.py
+++ b/solution.py
@@ -126,6 +126,10 @@
     one = jnp.zeros((1, mid), f32)
     two = jnp.zeros((1, mid), f32)
     for r in edges + inner:
+        if r == (edges + inner)[-1]:
+            pl.semaphore_wait(barrier, n - 1)
+            pl.when(has_up)(up_copies[0].start)
+            pl.when(has_down)(down_copies[0].start)
         x_copies[r].wait()
         value = dot(x_out[:, r].reshape(cells, ch), wr[...])
         first[r] = value
@@ -142,9 +146,8 @@
                 src[pl.ds(PIVOT_ROWS, cells), :] = sent
     pooled(st1, pivot, one, two)
 
-    pl.semaphore_wait(barrier, n - 1)
     copies1 = exchange_start(0, st1)
-    for c in range(chunks):
+    for c in range(1, chunks):
         pl.when(has_up)(up_copies[c].start)
         pl.when(has_down)(down_copies[c].start)
 
@@ -283,7 +286,7 @@
     imgs, rows, wid, ch = images.shape
     mid = w_reduce.shape[1]
     cells = imgs * wid
-    chunks = [imgs // 2, imgs - imgs // 2] if imgs > 1 else [imgs]
+    chunks = [1, imgs - 1] if imgs > 1 else [imgs]
     hbm = pl.BlockSpec(memory_space=pltpu.HBM)
     vmem = pl.BlockSpec(memory_space=pltpu.VMEM)
     vec = lambda c: pltpu.VMEM((1, c), f32)

time: 25.7 us -> 25.4 us (0.988)
  no operation moved by 1% of the time
where the time goes in v3:
time: 25.4 us; the launch traced here: 25.3 us
  Pallas kernels  25.3 us (100%)
    pallas_call x1, Pallas kernels, body(): pl.pallas_call(functools.partial(kernel, n, imgs, rows, wid, chunks), out...  23.6 us
    pallas_call x1, Pallas kernels, body(): pl.pallas_call(functools.partial(finish, pieces), out_shape=jax.ShapeDtyp...  1.67 us

profile of v3, /device:TPU:0, one launch (start us, length us, event | category | flops | bytes accessed | tf_op | source)
XLA Modules:
  0.0 25.3 jit_solution(1474583744847833601)
XLA Ops:
  0.0 0.0 copy-start
  0.0 23.6 %block_front.1 = (bf16[4,4,64,1024]{3,2,1,0:T(8,128)(2,1)S(1)}, f32[4,4,64,1024]{3,2,1,0:T(8,128)S(1)}, f32[2,1024]{1,0:T(2,128)S(1)}) custom-call(bf16[4,4,64,1024]{3,2,1,0:T(8,128)(2,1)} %images.1, bf16[1024,256]{1,0:T(8,128)(2,1)} %w_reduce.1, bf16[3,768,256]{2,1,0:T(8,128)(2,1)} %bitcast.13, bf16[256,1024]{1,0:T(8,128)(2,1)} %w_expand.1, ...), custom_call_target="tpu_custom_call" | custom-call | tf_op jit(solution)/shard_map/block_front/pallas_call | solution.py:295
  23.6 0.0 copy-done
  23.6 1.7 %block_finish.1 = bf16[1024,1024]{1,0:T(8,128)(2,1)} custom-call(f32[1024,1024]{1,0:T(8,128)S(1)} %bitcast.10, bf16[1024,1024]{1,0:T(8,128)(2,1)S(1)} %bitcast.11, f32[2,1024]{1,0:T(2,128)S(1)} %get-tuple-element.10.coef, f32[1,1024]{1,0:T(1,128)S(1)} %bitcast.12), custom_call_target="tpu_custom_call" | custom-call | tf_op jit(solution)/shard_map/block_finish/pallas_call | solution.py:335
Async XLA Ops:
  0.0 23.6 %copy-start = (f32[1024]{0:T(1024)S(1)}, f32[1024]{0:T(1024)}, u32[]{:S(2)}) copy-start(f32[1024]{0:T(1024)} %param.19) | copy-start | bytes 12292
